TPU v7x, 32 devices: a whole 2x2x4 slice. The times are simulated.
32 devices in a mesh: gx: 4 (over z), gy: 4 (over y, x), gz: 2 (over core).
Axes of the slice: x: 2, y: 2, z: 4, core: 2. Of those that a mesh axis runs over, the one named last changes fastest.
Arguments:
- volume: float32 [32, 256, 4096], P('gz', 'gy', 'gx'), may hold values from -24 to 24
Outputs:
- level_one: float32 [16, 128, 2048], P('gz', 'gy', 'gx')
- level_two: float32 [8, 64, 1024], P('gz', 'gy', 'gx')
- level_three: float32 [4, 32, 512], P('gz', 'gy', 'gx')
All inputs are finite; a program needn't handle non-finite values.
Results may differ from a plain program's by a relative error of at most 0.00002.
Values sent between devices are 32-bit elements; how exact they have to be, the bound alone decides.
A program may use at most 64 MiB of HBM per device.

v0:
```python
import jax
import jax.numpy as jnp
from jax import lax
from jax.sharding import PartitionSpec as P

taps = (0.0625, 0.25, 0.375, 0.25, 0.0625)


def extended(cells, sides, width):
    for axis, dim in sides:
        count = lax.axis_size(axis)
        ends = count - 1
        head = lax.slice_in_dim(cells, 0, width, axis=dim)
        tail = lax.slice_in_dim(cells, cells.shape[dim] - width, cells.shape[dim], axis=dim)
        cells = jnp.concatenate(
            [
                lax.ppermute(tail, axis, [(i, (i + 1) % count) for i in range(ends)]),
                cells,
                lax.ppermute(head, axis, [((i + 1) % count, i) for i in range(ends)]),
            ],
            axis=dim,
        )
    return cells


def reduce_padded(padded, dim, count):
    total = None
    for k in range(5):
        piece = lax.slice_in_dim(padded, k, k + 2 * count - 1, 2, dim)
        term = taps[k] * piece
        total = term if total is None else total + term
    return total


def pass_sections(block):
    padded = extended(block, (("gz", 0),), 2)
    return reduce_padded(padded, 0, block.shape[0] // 2)


def pass_rows(block):
    padded = extended(block, (("gy", 1),), 2)
    return reduce_padded(padded, 1, block.shape[1] // 2)


def pass_columns(block):
    padded = extended(block, (("gx", 2),), 2)
    return reduce_padded(padded, 2, block.shape[2] // 2)


def pass_whole_column(block):
    whole = lax.all_gather(block, "gz", axis=0, tiled=True)
    padded = jnp.pad(whole, ((2, 2), (0, 0), (0, 0)))
    reduced = reduce_padded(padded, 0, whole.shape[0] // 2)
    count = block.shape[0] // 2
    start = lax.axis_index("gz") * count
    return lax.dynamic_slice_in_dim(reduced, start, count, 0)


def level_down(block, final):
    section_pass = pass_whole_column if final else pass_sections
    return pass_columns(pass_rows(section_pass(block)))


def on_device(volume):
    level_one = level_down(volume, False)
    level_two = level_down(level_one, False)
    level_three = level_down(level_two, True)
    return (level_one, level_two, level_three)


def solution(mesh):
    in_specs = (P("gz", "gy", "gx"),)
    out_specs = (P("gz", "gy", "gx"), P("gz", "gy", "gx"), P("gz", "gy", "gx"))
    return jax.shard_map(
        on_device, mesh=mesh, in_specs=in_specs, out_specs=out_specs, check_vma=False
    )
```

profile of v0, /device:TPU:0, one launch (start us, length us, event | category | flops | bytes accessed | tf_op | source)
XLA Modules:
  0.0 194.8 jit_solution(1794749784522065808)
XLA Ops:
  0.6 1.3 fusion.4
  1.9 2.4 %collective-permute-start = (f32[2,64,1024]{2,1,0:T(8,128)S(1)}, f32[2,64,1024]{2,1,0:T(8,128)S(1)}, u32[]{:S(2)}, u32[]{:S(2)}) collective-permute-start(f32[2,64,1024]{2,1,0:T(8,128)S(1)} %get-tuple-element.4), channel_id=1, source_target_pairs={{0,1},{2,3},{4,5},{6,7},{8,9},{10,11},{12,13},{14,15},{16,17},{18,... | collective-permute-start | bytes 1572872 | tf_op jit(solution)/shard_map/ppermute | solution.py:17
  4.4 1.3 collective-permute-start.1
  5.7 0.2 collective-permute-done
  5.9 2.7 %constant_dynamic-update-slice_fusion.1 = f32[20,64,1024]{2,1,0:T(8,128)S(1)} fusion(f32[20,64,1024]{2,1,0:T(8,128)S(1)} %constant_dynamic-update-slice_fusion.2, f32[16,64,1024]{2,1,0:T(8,128)} %param.1), kind=kLoop, calls=%fused_computation.28 | loop fusion | bytes 8388608
  8.6 0.7 copy-done
  9.3 1.1 multiply_add_fusion
  10.4 0.1 fusion.5
  10.5 4.2 %collective-permute-start.2 = (f32[8,2,1024]{2,1,0:T(2,128)S(1)}, f32[8,2,1024]{2,1,0:T(2,128)S(1)}, u32[]{:S(2)}, u32[]{:S(2)}) collective-permute-start(f32[8,2,1024]{2,1,0:T(2,128)S(1)} %get-tuple-element.5), channel_id=1, source_target_pairs={{0,2},{2,4},{4,6},{1,3},{3,5},{5,7},{8,10},{10,12},{12,14},{9,11},... | collective-permute-start | bytes 196616 | tf_op jit(solution)/shard_map/ppermute | solution.py:17
  14.7 1.3 collective-permute-start.3
  16.0 0.5 slice.194
  16.5 2.8 %slice.195 = f32[8,32,1024]{2,1,0:T(8,128)} slice(f32[8,64,1024]{2,1,0:T(8,128)S(1)} %multiply_add_fusion), slice={[0:8:1], [1:64:2], [0:1024:1]} | slice | bytes 2097152 | tf_op jit(solution)/shard_map/slice | solution.py:29
  19.3 2.0 %collective-permute-done.3 = f32[8,2,1024]{2,1,0:T(2,128)S(1)} collective-permute-done((f32[8,2,1024]{2,1,0:T(2,128)S(1)}, f32[8,2,1024]{2,1,0:T(2,128)S(1)}, u32[]{:S(2)}, u32[]{:S(2)}) %collective-permute-start.3) | collective-permute-done | bytes 65568 | tf_op jit(solution)/shard_map/ppermute | solution.py:19
  21.3 1.8 pad_maximum_fusion
  23.0 5.4 %slice.192 = f32[8,32,1024]{2,1,0:T(8,128)} slice(f32[8,68,1024]{2,1,0:T(8,128)} %pad_maximum_fusion), slice={[0:8:1], [0:63:2], [0:1024:1]} | slice | bytes 2097152 | tf_op jit(solution)/shard_map/slice | solution.py:29
  28.4 5.5 %slice.193 = f32[8,32,1024]{2,1,0:T(8,128)} slice(f32[8,68,1024]{2,1,0:T(8,128)} %pad_maximum_fusion), slice={[0:8:1], [1:64:2], [0:1024:1]} | slice | bytes 2097152 | tf_op jit(solution)/shard_map/slice | solution.py:29
  34.0 5.5 %slice.196 = f32[8,32,1024]{2,1,0:T(8,128)} slice(f32[8,68,1024]{2,1,0:T(8,128)} %pad_maximum_fusion), slice={[0:8:1], [4:67:2], [0:1024:1]} | slice | bytes 2097152 | tf_op jit(solution)/shard_map/slice | solution.py:29
  39.4 2.4 %multiply_add_fusion.1 = f32[8,32,1024]{2,1,0:T(8,128)S(1)} fusion(f32[8,32,1024]{2,1,0:T(8,128)} %slice.196, f32[8,32,1024]{2,1,0:T(8,128)S(1)} %copy-done.2, f32[8,32,1024]{2,1,0:T(8,128)S(1)} %slice.194, f32[8,32,1024]{2,1,0:T(8,128)} %slice.193, f32[8,32,1024]{2,1,0:T(8,128)} %slice.192), kind=kLoop, calls=%fused_computation.2 | loop fusion | flops 2359296 | bytes 6291456 | tf_op jit(solution)/shard_map/add | solution.py:31
  41.9 0.1 fusion.6
  42.0 3.5 %collective-permute-start.4 = (f32[8,32,2]{2,1,0:T(8,128)S(1)}, f32[8,32,2]{2,1,0:T(8,128)S(1)}, u32[]{:S(2)}, u32[]{:S(2)}) collective-permute-start(f32[8,32,2]{2,1,0:T(8,128)S(1)} %get-tuple-element.8), channel_id=1, source_target_pairs={{0,8},{8,16},{16,24},{1,9},{9,17},{17,25},{2,10},{10,18},{18,26},{... | collective-permute-start | bytes 6152 | tf_op jit(solution)/shard_map/ppermute | solution.py:17
  45.5 1.5 collective-permute-start.5
  47.0 17.6 %slice.201 = f32[8,32,512]{2,1,0:T(8,128)S(1)} slice(f32[8,32,1024]{2,1,0:T(8,128)S(1)} %multiply_add_fusion.1), slice={[0:8:1], [0:32:1], [0:1023:2]} | slice | bytes 1048576 | tf_op jit(solution)/shard_map/slice | solution.py:29
  64.5 17.6 %slice.202 = f32[8,32,512]{2,1,0:T(8,128)S(1)} slice(f32[8,32,1024]{2,1,0:T(8,128)S(1)} %multiply_add_fusion.1), slice={[0:8:1], [0:32:1], [1:1024:2]} | slice | bytes 1048576 | tf_op jit(solution)/shard_map/slice | solution.py:29
  82.1 0.8 concatenate.26
  82.9 17.6 %slice.199 = f32[8,32,512]{2,1,0:T(8,128)S(1)} slice(f32[8,32,1028]{2,1,0:T(8,128)S(1)} %concatenate.26), slice={[0:8:1], [0:32:1], [0:1023:2]} | slice | bytes 1048576 | tf_op jit(solution)/shard_map/slice | solution.py:29
  100.5 18.4 %slice.200 = f32[8,32,512]{2,1,0:T(8,128)} slice(f32[8,32,1028]{2,1,0:T(8,128)S(1)} %concatenate.26), slice={[0:8:1], [0:32:1], [1:1024:2]} | slice | bytes 1048576 | tf_op jit(solution)/shard_map/slice | solution.py:29
  118.9 18.2 %slice.203 = f32[8,32,512]{2,1,0:T(8,128)} slice(f32[8,32,1028]{2,1,0:T(8,128)S(1)} %concatenate.26), slice={[0:8:1], [0:32:1], [4:1027:2]} | slice | bytes 1048576 | tf_op jit(solution)/shard_map/slice | solution.py:29
  137.1 1.5 multiply_add_fusion.2
  138.6 1.5 collective-permute-start.6
  140.1 1.3 collective-permute-start.7
  141.4 1.9 collective-permute-done.7
  143.3 0.1 pad_maximum_fusion.1
  143.4 0.1 multiply_add_fusion.3
  143.6 4.3 %collective-permute-start.8 = (f32[4,2,512]{2,1,0:T(2,128)S(1)}, f32[4,2,512]{2,1,0:T(2,128)S(1)}, u32[]{:S(2)}, u32[]{:S(2)}) collective-permute-start(f32[4,2,512]{2,1,0:T(2,128)S(1)} %get-tuple-element.11), channel_id=1, source_target_pairs={{0,2},{2,4},{4,6},{1,3},{3,5},{5,7},{8,10},{10,12},{12,14},{9,11},... | collective-permute-start | bytes 49160 | tf_op jit(solution)/shard_map/ppermute | solution.py:17
  147.9 1.3 collective-permute-start.9
  149.3 0.0 collective-permute-done.8
  149.3 4.2 %collective-permute-done.9 = f32[4,2,512]{2,1,0:T(2,128)S(1)} collective-permute-done((f32[4,2,512]{2,1,0:T(2,128)S(1)}, f32[4,2,512]{2,1,0:T(2,128)S(1)}, u32[]{:S(2)}, u32[]{:S(2)}) %collective-permute-start.9) | collective-permute-done | bytes 16416 | tf_op jit(solution)/shard_map/ppermute | solution.py:19
  153.6 0.1 slice.217
  153.7 0.1 multiply_add_fusion.4
  153.8 0.1 fusion.9
  153.9 4.4 %collective-permute-start.10 = (f32[4,16,2]{2,1,0:T(8,128)S(1)}, f32[4,16,2]{2,1,0:T(8,128)S(1)}, u32[]{:S(2)}, u32[]{:S(2)}) collective-permute-start(f32[4,16,2]{2,1,0:T(8,128)S(1)} %get-tuple-element.18), channel_id=1, source_target_pairs={{0,8},{8,16},{16,24},{1,9},{9,17},{17,25},{2,10},{10,18},{18,26},{... | collective-permute-start | bytes 1544 | tf_op jit(solution)/shard_map/ppermute | solution.py:17
  158.2 1.6 collective-permute-start.11
  159.8 2.2 %slice.222 = f32[4,16,256]{2,1,0:T(8,128)S(1)} slice(f32[4,16,512]{2,1,0:T(8,128)S(1)} %multiply_add_fusion.4), slice={[0:4:1], [0:16:1], [0:511:2]} | slice | bytes 131072 | tf_op jit(solution)/shard_map/slice | solution.py:29
  162.0 2.2 %slice.223 = f32[4,16,256]{2,1,0:T(8,128)S(1)} slice(f32[4,16,512]{2,1,0:T(8,128)S(1)} %multiply_add_fusion.4), slice={[0:4:1], [0:16:1], [1:512:2]} | slice | bytes 131072 | tf_op jit(solution)/shard_map/slice | solution.py:29
  164.2 0.1 pad_maximum_fusion.3
  164.4 2.2 %slice.220 = f32[4,16,256]{2,1,0:T(8,128)S(1)} slice(f32[4,16,516]{2,1,0:T(8,128)S(1)} %pad_maximum_fusion.3), slice={[0:4:1], [0:16:1], [0:511:2]} | slice | bytes 131072 | tf_op jit(solution)/shard_map/slice | solution.py:29
  166.6 2.2 %slice.221 = f32[4,16,256]{2,1,0:T(8,128)S(1)} slice(f32[4,16,516]{2,1,0:T(8,128)S(1)} %pad_maximum_fusion.3), slice={[0:4:1], [0:16:1], [1:512:2]} | slice | bytes 131072 | tf_op jit(solution)/shard_map/slice | solution.py:29
  168.8 2.2 %slice.224 = f32[4,16,256]{2,1,0:T(8,128)S(1)} slice(f32[4,16,516]{2,1,0:T(8,128)S(1)} %pad_maximum_fusion.3), slice={[0:4:1], [0:16:1], [4:515:2]} | slice | bytes 131072 | tf_op jit(solution)/shard_map/slice | solution.py:29
  171.0 0.0 copy-start.3
  171.1 1.9 all_gather.3
  173.0 4.0 %collective-permute-start.12 = (f32[2,2,256]{2,1,0:T(2,128)S(1)}, f32[2,2,256]{2,1,0:T(2,128)S(1)}, u32[]{:S(2)}, u32[]{:S(2)}) collective-permute-start(f32[2,2,256]{2,1,0:T(2,128)S(1)} %get-tuple-element.20), channel_id=1, source_target_pairs={{0,2},{2,4},{4,6},{1,3},{3,5},{5,7},{8,10},{10,12},{12,14},{9,11},... | collective-permute-start | bytes 12296 | tf_op jit(solution)/shard_map/ppermute | solution.py:17
  177.0 1.3 collective-permute-start.13
  178.4 4.2 %collective-permute-done.13 = f32[2,2,256]{2,1,0:T(2,128)S(1)} collective-permute-done((f32[2,2,256]{2,1,0:T(2,128)S(1)}, f32[2,2,256]{2,1,0:T(2,128)S(1)}, u32[]{:S(2)}, u32[]{:S(2)}) %collective-permute-start.13) | collective-permute-done | bytes 4128 | tf_op jit(solution)/shard_map/ppermute | solution.py:19
  182.6 0.1 fusion.11
  182.7 0.3 slice.241
  183.0 4.5 %collective-permute-start.14 = (f32[2,8,2]{2,1,0:T(8,128)S(1)}, f32[2,8,2]{2,1,0:T(8,128)S(1)}, u32[]{:S(2)}, u32[]{:S(2)}) collective-permute-start(f32[2,8,2]{2,1,0:T(8,128)S(1)} %get-tuple-element.22), channel_id=1, source_target_pairs={{0,8},{8,16},{16,24},{1,9},{9,17},{17,25},{2,10},{10,18},{18,26},{... | collective-permute-start | bytes 392 | tf_op jit(solution)/shard_map/ppermute | solution.py:17
  187.6 1.3 collective-permute-start.15
  188.9 0.3 slice.242
  189.2 3.9 %collective-permute-done.15 = f32[2,8,2]{2,1,0:T(8,128)S(1)} collective-permute-done((f32[2,8,2]{2,1,0:T(8,128)S(1)}, f32[2,8,2]{2,1,0:T(8,128)S(1)}, u32[]{:S(2)}, u32[]{:S(2)}) %collective-permute-start.15) | collective-permute-done | bytes 160 | tf_op jit(solution)/shard_map/ppermute | solution.py:19
  193.1 0.1 pad_maximum_fusion.5
  193.2 0.3 slice.239
  193.5 0.3 slice.240
  193.9 0.3 slice.243
  194.2 0.6 multiply_add_fusion.7
  (35 shorter events, 0.6 us)
Async XLA Ops:
  1.9 3.9 %collective-permute-start = (f32[2,64,1024]{2,1,0:T(8,128)S(1)}, f32[2,64,1024]{2,1,0:T(8,128)S(1)}, u32[]{:S(2)}, u32[]{:S(2)}) collective-permute-start(f32[2,64,1024]{2,1,0:T(8,128)S(1)} %get-tuple-element.4), channel_id=1, source_target_pairs={{0,1},{2,3},{4,5},{6,7},{8,9},{10,11},{12,13},{14,15},{16,17},{18,... | collective-permute-start | bytes 1572872 | tf_op jit(solution)/shard_map/ppermute | solution.py:17
  4.4 4.2 %collective-permute-start.1 = (f32[2,64,1024]{2,1,0:T(8,128)S(1)}, f32[2,64,1024]{2,1,0:T(8,128)S(1)}, u32[]{:S(2)}, u32[]{:S(2)}) collective-permute-start(f32[2,64,1024]{2,1,0:T(8,128)S(1)} %get-tuple-element.3), channel_id=1, source_target_pairs={{1,0},{3,2},{5,4},{7,6},{9,8},{11,10},{13,12},{15,14},{17,16},{19,... | collective-permute-start | bytes 1572872 | tf_op jit(solution)/shard_map/ppermute | solution.py:19
  5.9 3.5 %copy-start = (f32[16,64,1024]{2,1,0:T(8,128)S(1)}, f32[16,64,1024]{2,1,0:T(8,128)}, u32[]{:S(2)}) copy-start(f32[16,64,1024]{2,1,0:T(8,128)} %param.1) | copy-start | bytes 12582916
  10.5 8.9 %collective-permute-start.2 = (f32[8,2,1024]{2,1,0:T(2,128)S(1)}, f32[8,2,1024]{2,1,0:T(2,128)S(1)}, u32[]{:S(2)}, u32[]{:S(2)}) collective-permute-start(f32[8,2,1024]{2,1,0:T(2,128)S(1)} %get-tuple-element.5), channel_id=1, source_target_pairs={{0,2},{2,4},{4,6},{1,3},{3,5},{5,7},{8,10},{10,12},{12,14},{9,11},... | collective-permute-start | bytes 196616 | tf_op jit(solution)/shard_map/ppermute | solution.py:17
  14.7 6.6 %collective-permute-start.3 = (f32[8,2,1024]{2,1,0:T(2,128)S(1)}, f32[8,2,1024]{2,1,0:T(2,128)S(1)}, u32[]{:S(2)}, u32[]{:S(2)}) collective-permute-start(f32[8,2,1024]{2,1,0:T(2,128)S(1)} %get-tuple-element.6), channel_id=1, source_target_pairs={{2,0},{4,2},{6,4},{3,1},{5,3},{7,5},{10,8},{12,10},{14,12},{11,9},... | collective-permute-start | bytes 196616 | tf_op jit(solution)/shard_map/ppermute | solution.py:19
  28.4 11.0 %copy-start.2 = (f32[8,32,1024]{2,1,0:T(8,128)S(1)}, f32[8,32,1024]{2,1,0:T(8,128)}, u32[]{:S(2)}) copy-start(f32[8,32,1024]{2,1,0:T(8,128)} %slice.195) | copy-start | bytes 3145732
  42.0 40.1 %collective-permute-start.4 = (f32[8,32,2]{2,1,0:T(8,128)S(1)}, f32[8,32,2]{2,1,0:T(8,128)S(1)}, u32[]{:S(2)}, u32[]{:S(2)}) collective-permute-start(f32[8,32,2]{2,1,0:T(8,128)S(1)} %get-tuple-element.8), channel_id=1, source_target_pairs={{0,8},{8,16},{16,24},{1,9},{9,17},{17,25},{2,10},{10,18},{18,26},{... | collective-permute-start | bytes 6152 | tf_op jit(solution)/shard_map/ppermute | solution.py:17
  45.5 36.7 %collective-permute-start.5 = (f32[8,32,2]{2,1,0:T(8,128)S(1)}, f32[8,32,2]{2,1,0:T(8,128)S(1)}, u32[]{:S(2)}, u32[]{:S(2)}) collective-permute-start(f32[8,32,2]{2,1,0:T(8,128)S(1)} %get-tuple-element.7), channel_id=1, source_target_pairs={{8,0},{16,8},{24,16},{9,1},{17,9},{25,17},{10,2},{18,10},{26,18},{... | collective-permute-start | bytes 6152 | tf_op jit(solution)/shard_map/ppermute | solution.py:19
  138.6 10.7 %copy-start.1 = (f32[8,32,512]{2,1,0:T(8,128)}, f32[8,32,512]{2,1,0:T(8,128)S(1)}, u32[]{:S(2)}) copy-start(f32[8,32,512]{2,1,0:T(8,128)S(1)} %multiply_add_fusion.2) | copy-start | bytes 1572868
  138.6 2.8 %collective-permute-start.6 = (f32[2,32,512]{2,1,0:T(8,128)S(1)}, f32[2,32,512]{2,1,0:T(8,128)S(1)}, u32[]{:S(2)}, u32[]{:S(2)}) collective-permute-start(f32[2,32,512]{2,1,0:T(8,128)S(1)} %get-tuple-element.9), channel_id=1, source_target_pairs={{0,1},{2,3},{4,5},{6,7},{8,9},{10,11},{12,13},{14,15},{16,17},{18,... | collective-permute-start | bytes 393224 | tf_op jit(solution)/shard_map/ppermute | solution.py:17
  140.1 3.2 %collective-permute-start.7 = (f32[2,32,512]{2,1,0:T(8,128)S(1)}, f32[2,32,512]{2,1,0:T(8,128)S(1)}, u32[]{:S(2)}, u32[]{:S(2)}) collective-permute-start(f32[2,32,512]{2,1,0:T(8,128)S(1)} %get-tuple-element.10), channel_id=1, source_target_pairs={{1,0},{3,2},{5,4},{7,6},{9,8},{11,10},{13,12},{15,14},{17,16},{19,... | collective-permute-start | bytes 393224 | tf_op jit(solution)/shard_map/ppermute | solution.py:19
  143.6 5.7 %collective-permute-start.8 = (f32[4,2,512]{2,1,0:T(2,128)S(1)}, f32[4,2,512]{2,1,0:T(2,128)S(1)}, u32[]{:S(2)}, u32[]{:S(2)}) collective-permute-start(f32[4,2,512]{2,1,0:T(2,128)S(1)} %get-tuple-element.11), channel_id=1, source_target_pairs={{0,2},{2,4},{4,6},{1,3},{3,5},{5,7},{8,10},{10,12},{12,14},{9,11},... | collective-permute-start | bytes 49160 | tf_op jit(solution)/shard_map/ppermute | solution.py:17
  147.9 5.6 %collective-permute-start.9 = (f32[4,2,512]{2,1,0:T(2,128)S(1)}, f32[4,2,512]{2,1,0:T(2,128)S(1)}, u32[]{:S(2)}, u32[]{:S(2)}) collective-permute-start(f32[4,2,512]{2,1,0:T(2,128)S(1)} %get-tuple-element.12), channel_id=1, source_target_pairs={{2,0},{4,2},{6,4},{3,1},{5,3},{7,5},{10,8},{12,10},{14,12},{11,9},... | collective-permute-start | bytes 49160 | tf_op jit(solution)/shard_map/ppermute | solution.py:19
  153.9 10.4 %collective-permute-start.10 = (f32[4,16,2]{2,1,0:T(8,128)S(1)}, f32[4,16,2]{2,1,0:T(8,128)S(1)}, u32[]{:S(2)}, u32[]{:S(2)}) collective-permute-start(f32[4,16,2]{2,1,0:T(8,128)S(1)} %get-tuple-element.18), channel_id=1, source_target_pairs={{0,8},{8,16},{16,24},{1,9},{9,17},{17,25},{2,10},{10,18},{18,26},{... | collective-permute-start | bytes 1544 | tf_op jit(solution)/shard_map/ppermute | solution.py:17
  158.2 6.0 %collective-permute-start.11 = (f32[4,16,2]{2,1,0:T(8,128)S(1)}, f32[4,16,2]{2,1,0:T(8,128)S(1)}, u32[]{:S(2)}, u32[]{:S(2)}) collective-permute-start(f32[4,16,2]{2,1,0:T(8,128)S(1)} %get-tuple-element.19), channel_id=1, source_target_pairs={{8,0},{16,8},{24,16},{9,1},{17,9},{25,17},{10,2},{18,10},{26,18},{... | collective-permute-start | bytes 1544 | tf_op jit(solution)/shard_map/ppermute | solution.py:19
  171.0 23.8 %copy-start.3 = (f32[4,16,256]{2,1,0:T(8,128)}, f32[4,16,256]{2,1,0:T(8,128)S(1)}, u32[]{:S(2)}) copy-start(f32[4,16,256]{2,1,0:T(8,128)S(1)} %multiply_add_fusion.5) | copy-start | bytes 196612
  173.0 5.3 %collective-permute-start.12 = (f32[2,2,256]{2,1,0:T(2,128)S(1)}, f32[2,2,256]{2,1,0:T(2,128)S(1)}, u32[]{:S(2)}, u32[]{:S(2)}) collective-permute-start(f32[2,2,256]{2,1,0:T(2,128)S(1)} %get-tuple-element.20), channel_id=1, source_target_pairs={{0,2},{2,4},{4,6},{1,3},{3,5},{5,7},{8,10},{10,12},{12,14},{9,11},... | collective-permute-start | bytes 12296 | tf_op jit(solution)/shard_map/ppermute | solution.py:17
  177.0 5.5 %collective-permute-start.13 = (f32[2,2,256]{2,1,0:T(2,128)S(1)}, f32[2,2,256]{2,1,0:T(2,128)S(1)}, u32[]{:S(2)}, u32[]{:S(2)}) collective-permute-start(f32[2,2,256]{2,1,0:T(2,128)S(1)} %get-tuple-element.21), channel_id=1, source_target_pairs={{2,0},{4,2},{6,4},{3,1},{5,3},{7,5},{10,8},{12,10},{14,12},{11,9},... | collective-permute-start | bytes 12296 | tf_op jit(solution)/shard_map/ppermute | solution.py:19
  183.0 6.2 %collective-permute-start.14 = (f32[2,8,2]{2,1,0:T(8,128)S(1)}, f32[2,8,2]{2,1,0:T(8,128)S(1)}, u32[]{:S(2)}, u32[]{:S(2)}) collective-permute-start(f32[2,8,2]{2,1,0:T(8,128)S(1)} %get-tuple-element.22), channel_id=1, source_target_pairs={{0,8},{8,16},{16,24},{1,9},{9,17},{17,25},{2,10},{10,18},{18,26},{... | collective-permute-start | bytes 392 | tf_op jit(solution)/shard_map/ppermute | solution.py:17
  187.6 5.5 %collective-permute-start.15 = (f32[2,8,2]{2,1,0:T(8,128)S(1)}, f32[2,8,2]{2,1,0:T(8,128)S(1)}, u32[]{:S(2)}, u32[]{:S(2)}) collective-permute-start(f32[2,8,2]{2,1,0:T(8,128)S(1)} %get-tuple-element.23), channel_id=1, source_target_pairs={{8,0},{16,8},{24,16},{9,1},{17,9},{25,17},{10,2},{18,10},{26,18},{... | collective-permute-start | bytes 392 | tf_op jit(solution)/shard_map/ppermute | solution.py:19
where the time goes:
time: 196 us; the launch traced here: 195 us
  local copies, waits for them, and re-layouts  128 us (65%)
  starting transfers between devices  39.6 us (20%)
  waiting for transfers between devices  16.4 us (8%)
  other arithmetic  7.93 us (4%)
    slice x31, local copies, waits for them, and re-layouts, reduce_padded(): piece = lax.slice_in_dim(padded, k, k + 2 * count - 1, 2, dim)  122 us
    ppermute x8, starting transfers between devices, extended(): lax.ppermute(tail, axis, [(i, (i + 1) % count) for i in range(ends)])  28.8 us
    ppermute x8, waiting for transfers between devices, extended(): lax.ppermute(head, axis, [((i + 1) % count, i) for i in range(ends)])  16.2 us
    ppermute x8, starting transfers between devices, extended(): lax.ppermute(head, axis, [((i + 1) % count, i) for i in range(ends)])  10.8 us
    add x9, other arithmetic, reduce_padded(): total = term if total is None else total + term  5.87 us
  transfers between devices with their start and end apart: 16, of which 6 were waited for; matrix products, arithmetic and copies ran while one was open for 24% of the time, Pallas kernels for 0%

commit v1 on v0

v1 whole, which is shorter than its diff:
```python
import functools

import jax
import jax.numpy as jnp
from jax import lax
from jax.experimental import pallas as pl
from jax.experimental.pallas import tpu as pltpu
from jax.sharding import PartitionSpec as P

LANES = 128
MESH = pl.DeviceIdType.MESH
AXES = ("gz", "gy", "gx")
W0, W1, W2 = 0.0625, 0.25, 0.375


def taps_of(delta):
    far = jnp.abs(delta)
    return jnp.where(
        far == 0, W2, jnp.where(far == 1, W1, jnp.where(far == 2, W0, 0.0))
    ).astype(jnp.bfloat16)


def column_weights():
    row = lax.broadcasted_iota(jnp.int32, (LANES, LANES), 0)
    col = lax.broadcasted_iota(jnp.int32, (LANES, LANES), 1)
    before = taps_of(row - LANES - 2 * col)
    first = taps_of(row - 2 * col)
    second = taps_of(row + LANES - 2 * col)
    after = taps_of(row + 2 * LANES - 2 * col)
    half = LANES // 2
    signed_in = jnp.where(row < half, row, row - LANES)
    signed_out = jnp.where(col < half, col, col - LANES)
    same_side = (row < half) == (col < half)
    halo = taps_of(jnp.where(same_side, signed_in - 2 * signed_out, LANES))
    return before, first, second, after, halo


def split3(x):
    hi = x.astype(jnp.bfloat16)
    rest = x - hi.astype(jnp.float32)
    mid = rest.astype(jnp.bfloat16)
    lo = (rest - mid.astype(jnp.float32)).astype(jnp.bfloat16)
    return hi, mid, lo


def dots(tiles, weights):
    parts = [split3(t) for t in tiles]
    total = None
    for p in (2, 1, 0):
        lhs = jnp.concatenate([q[p] for q in parts], axis=1)
        d = jnp.dot(lhs, weights, preferred_element_type=jnp.float32)
        total = d if total is None else total + d
    return total


def kernel(sizes, nz, ny, nt, vol, out1, out2, out3,
           v, z1, z2, z3, l1, l2,
           ys_lo, ys_hi, yr_lo, yr_hi,
           t1, t2, t3, xs_lo, xs_hi, xr, wm, wh,
           load_sem, zsend, zrecv, ysend, yrecv, xsend, xrecv):
    idx = {a: lax.axis_index(a) for a in AXES}
    has_lo = {a: idx[a] > 0 for a in AXES}
    has_hi = {a: idx[a] < sizes[a] - 1 for a in AXES}
    below = {a: {a: jnp.maximum(idx[a] - 1, 0)} for a in AXES}
    above = {a: {a: jnp.minimum(idx[a] + 1, sizes[a] - 1)} for a in AXES}

    xr[...] = jnp.zeros(xr.shape, jnp.float32)
    barrier = pltpu.get_barrier_semaphore()
    for a in AXES:
        @pl.when(has_lo[a])
        def _():
            pl.semaphore_signal(barrier, inc=1, device_id=below[a], device_id_type=MESH)

        @pl.when(has_hi[a])
        def _():
            pl.semaphore_signal(barrier, inc=1, device_id=above[a], device_id_type=MESH)

    groups = ((0, 8), (ny - 8, 8), (8, ny - 16))
    loads = []
    for g, (r0, rn) in enumerate(groups):
        c = pltpu.make_async_copy(
            vol.at[:, pl.ds(r0, rn), :], v.at[pl.ds(2, nz), pl.ds(r0, rn), :], load_sem.at[g])
        c.start()
        loads.append(c)

    for z, lev in ((v, 0), (l1, 1), (l2, 2)):
        @pl.when(jnp.logical_not(has_lo["gz"]))
        def _():
            z[0:2] = jnp.zeros((2,) + z.shape[1:], jnp.float32)

        @pl.when(jnp.logical_not(has_hi["gz"]))
        def _():
            n = z.shape[0]
            z[n - 1:n] = jnp.zeros((1,) + z.shape[1:], jnp.float32)
    for lev in range(3):
        @pl.when(jnp.logical_not(has_lo["gy"]))
        def _():
            yr_lo[lev][...] = jnp.zeros(yr_lo[lev].shape, jnp.float32)

        @pl.when(jnp.logical_not(has_hi["gy"]))
        def _():
            yr_hi[lev][...] = jnp.zeros(yr_hi[lev].shape, jnp.float32)
    before, first, second, after, halo = column_weights()
    for i, m in enumerate((before, first, second, after)):
        wm[i * LANES:(i + 1) * LANES] = m
    for i, m in enumerate((before, halo, after)):
        wh[i * LANES:(i + 1) * LANES] = m

    peers = sum(has_lo[a].astype(jnp.int32) + has_hi[a].astype(jnp.int32) for a in AXES)
    pl.semaphore_wait(barrier, peers)

    pending = []

    def exchange(axis, src_lo, dst_hi, src_hi, dst_lo, send, recv, base):
        down = pltpu.make_async_remote_copy(
            src_ref=src_lo, dst_ref=dst_hi, send_sem=send.at[base], recv_sem=recv.at[base],
            device_id=below[axis], device_id_type=MESH)
        up = pltpu.make_async_remote_copy(
            src_ref=src_hi, dst_ref=dst_lo, send_sem=send.at[base + 1],
            recv_sem=recv.at[base + 1], device_id=above[axis], device_id_type=MESH)

        @pl.when(has_hi[axis])
        def _():
            up.start()

        @pl.when(has_lo[axis])
        def _():
            down.start()

        pending.append((axis, down, up))

        def wait():
            @pl.when(has_lo[axis])
            def _():
                up.wait_recv()

            @pl.when(has_hi[axis])
            def _():
                down.wait_recv()

        return wait

    wait_z = exchange(
        "gz", vol.at[pl.ds(0, 1)], v.at[pl.ds(nz + 2, 1)],
        vol.at[pl.ds(nz - 2, 2)], v.at[pl.ds(0, 2)], zsend, zrecv, 0)

    def section_sum(load, s):
        return W0 * (load(2 * s) + load(2 * s + 4)) + W1 * (load(2 * s + 1) + load(2 * s + 3)) \
            + W2 * load(2 * s + 2)

    def sections_first(s, r0, rn):
        for r in range(r0, r0 + rn, 8):
            for lt in range(nt):
                cols = slice(lt * LANES, (lt + 1) * LANES)
                z1[s, lt, 8 + r:16 + r, :] = section_sum(lambda i: v[i, r:r + 8, cols], s)

    def sections_next(src, dst, s, tiles, rows):
        for lt in range(tiles):
            dst[s, lt, 8:8 + rows, :] = section_sum(lambda i: src[i, lt], s)

    def send_rows(lev, z, rows):
        ys_hi[lev][...] = z[:, :, 6 + rows:8 + rows, :]
        ys_lo[lev][...] = z[:, :, 8:9, :]
        return exchange("gy", ys_lo[lev], yr_hi[lev], ys_hi[lev], yr_lo[lev],
                        ysend, yrecv, 2 * lev)

    def take_rows(lev, z, rows):
        z[:, :, 6:8, :] = yr_lo[lev][...]
        z[:, :, 8 + rows:9 + rows, :] = yr_hi[lev][...]

    def row_sum(z, t, s, lt, rows):
        def load(k):
            return z[s, lt, pl.ds(6 + k, rows // 2, 2), :]
        t[lt, s] = W0 * (load(0) + load(4)) + W1 * (load(1) + load(3)) + W2 * load(2)

    def tile_of(t, i):
        x = t[i]
        return x.reshape(x.shape[0] * x.shape[1], LANES)

    def main_tile(t, j, tiles):
        ids = ((2 * j - 1) % (tiles + 1), 2 * j, 2 * j + 1, 2 * j + 2)
        return dots([tile_of(t, i) for i in ids], wm[...])

    def halo_tile(t, tiles):
        out = dots([tile_of(t, i) for i in (tiles - 1, tiles, 0)], wh[...])
        lane = lax.broadcasted_iota(jnp.int32, out.shape, 1)
        keep_hi = jnp.where(has_hi["gx"], 1, 0)
        keep_lo = jnp.where(has_lo["gx"], 1, 0)
        keep = jnp.where(lane < LANES // 2, keep_hi, keep_lo)
        return jnp.where(keep > 0, out, 0.0)

    def put(l, j, x):
        n = l.shape[0] - 3
        l[2:2 + n, j] = x.reshape(n, l.shape[2], LANES)

    nz1, ny1 = nz // 2, ny // 2
    loads[0].wait()
    loads[1].wait()

    def edges(s):
        sections_first(s, 0, 8)
        sections_first(s, ny - 8, 8)

    @pl.loop(1, nz1 - 1)
    def _(s):
        edges(s)
    wait_z()
    edges(0)
    edges(nz1 - 1)
    wait_y = send_rows(0, z1, ny)
    loads[2].wait()

    @pl.loop(0, nz1)
    def _(s):
        sections_first(s, 8, ny - 16)
    wait_y()
    take_rows(0, z1, ny)

    @pl.loop(0, nz1)
    def _(s):
        row_sum(z1, t1, s, 0, ny)
        row_sum(z1, t1, s, nt - 1, ny)
    xs_lo[...] = tile_of(t1, 0).T[0:8, :]
    xs_hi[...] = tile_of(t1, nt - 1).T[LANES - 16:LANES, :]
    wait_x = exchange("gx", xs_lo, xr.at[pl.ds(0, 8)], xs_hi, xr.at[pl.ds(LANES - 16, 16)],
                      xsend, xrecv, 0)

    @pl.loop(0, nz1)
    def _(s):
        for lt in range(1, nt - 1):
            row_sum(z1, t1, s, lt, ny)
    nt1 = nt // 2
    for j in range(1, nt1 - 1):
        put(l1, j, main_tile(t1, j, nt))
    wait_x()
    t1[nt] = xr[...].T.reshape(nz1, ny1, LANES)
    put(l1, 0, main_tile(t1, 0, nt))
    put(l1, nt1 - 1, main_tile(t1, nt1 - 1, nt))
    put(l1, nt1, halo_tile(t1, nt))

    def store(l, out, tiles):
        n = out.shape[0]
        for j in range(tiles):
            out[:, :, j * LANES:(j + 1) * LANES] = l[2:2 + n, j]

    def next_level(lev, src, z, t, rows, tiles):
        n = src.shape[0] - 3
        wait = exchange("gz", src.at[pl.ds(2, 1)], src.at[pl.ds(n + 2, 1)],
                        src.at[pl.ds(n, 2)], src.at[pl.ds(0, 2)], zsend, zrecv, 2 * lev)
        for s in range(1, n // 2 - 1):
            sections_next(src, z, s, tiles + 1, rows)
        wait()
        sections_next(src, z, 0, tiles + 1, rows)
        sections_next(src, z, n // 2 - 1, tiles + 1, rows)
        wait_rows = send_rows(lev, z, rows)
        return wait_rows

    def finish_rows(lev, wait_rows, z, t, rows, tiles):
        wait_rows()
        take_rows(lev, z, rows)
        for s in range(z.shape[0]):
            for lt in range(tiles + 1):
                row_sum(z, t, s, lt, rows)

    w = next_level(1, l1, z2, t2, ny1, nt1)
    store(l1, out1, nt1)
    finish_rows(1, w, z2, t2, ny1, nt1)
    nt2, ny2 = nt1 // 2, ny1 // 2
    for j in range(nt2):
        put(l2, j, main_tile(t2, j, nt1))
    put(l2, nt2, halo_tile(t2, nt1))

    w = next_level(2, l2, z3, t3, ny2, nt2)
    store(l2, out2, nt2)
    finish_rows(2, w, z3, t3, ny2, nt2)
    nt3 = nt2 // 2
    for j in range(nt3):
        x = main_tile(t3, j, nt2)
        out3[:, :, j * LANES:(j + 1) * LANES] = x.reshape(out3.shape[0], out3.shape[1], LANES)

    for axis, down, up in pending:
        @pl.when(has_lo[axis])
        def _():
            down.wait_send()

        @pl.when(has_hi[axis])
        def _():
            up.wait_send()


def on_device(sizes, volume):
    f32 = jnp.float32
    nz, ny, nx = volume.shape
    nt = nx // LANES
    V = pltpu.VMEM
    z = [V((nz >> (l + 1), (nt >> l) + (l > 0), (ny >> l) + 16, LANES), f32) for l in range(3)]
    lv = [V((3 + (nz >> l), (nt >> l) + 1, ny >> l, LANES), f32) for l in (1, 2)]
    halo = lambda k: [V((nz >> (l + 1), (nt >> l) + (l > 0), k, LANES), f32) for l in range(3)]
    t = [V(((nt >> l) + 1, nz >> (l + 1), ny >> (l + 1), LANES), f32) for l in range(3)]
    packed = (nz >> 1) * (ny >> 1)
    dma = pltpu.SemaphoreType.DMA
    hbm = pl.BlockSpec(memory_space=pltpu.HBM)
    vmem = pl.BlockSpec(memory_space=pltpu.VMEM)
    return pl.pallas_call(
        functools.partial(kernel, sizes, nz, ny, nt),
        out_shape=tuple(
            jax.ShapeDtypeStruct((nz >> l, ny >> l, nx >> l), f32) for l in (1, 2, 3)),
        in_specs=[hbm],
        out_specs=(vmem, vmem, vmem),
        scratch_shapes=[
            V((nz + 3, ny, nx), f32), *z, *lv,
            halo(1), halo(2), halo(2), halo(1),
            *t, V((8, packed), f32), V((16, packed), f32), V((LANES, packed), f32),
            V((4 * LANES, LANES), jnp.bfloat16), V((3 * LANES, LANES), jnp.bfloat16),
            dma((3,)),
            dma((6,)), dma((6,)), dma((6,)), dma((6,)), dma((2,)), dma((2,)),
        ],
        compiler_params=pltpu.CompilerParams(
            collective_id=0, has_side_effects=True, vmem_limit_bytes=61 << 20),
        name="pyramid",
    )(volume)


def solution(mesh):
    sizes = {a: mesh.shape[a] for a in AXES}
    spec = P(*AXES)
    return jax.shard_map(
        functools.partial(on_device, sizes), mesh=mesh, in_specs=(spec,),
        out_specs=(spec, spec, spec), check_vma=False)
```

time: 196 us -> 27 us (0.14)
  local copies, waits for them, and re-layouts: 128 us -> 4.64 us
  starting transfers between devices: 39.6 us -> 0 us
  Pallas kernels: 0 us -> 21.5 us
  waiting for transfers between devices: 16.4 us -> 0 us
  other arithmetic: 7.93 us -> 0 us
    slice x39 -> x0, local copies, waits for them, and re-layouts: 124 us -> none  [the longest x31 122 us: reduce_padded(): piece = lax.slice_in_dim(padded, k, k + 2 * count - 1, 2, dim)]
    ppermute x16 -> x0, starting transfers between devices: 39.6 us -> none  [the longest x8 28.8 us: extended(): lax.ppermute(tail, axis, [(i, (i + 1) % count) for i in range(ends)])]
    pallas_call x0 -> x1, Pallas kernels: none -> 21.5 us  [on_device(): pl.pallas_call(functools.partial(kernel, sizes, nz, ny, nt), out_shape=tu...]
    ppermute x16 -> x0, waiting for transfers between devices: 16.4 us -> none  [the longest x8 16.2 us: extended(): lax.ppermute(head, axis, [((i + 1) % count, i) for i in range(ends)])]
    add x9 -> x0, other arithmetic: 5.87 us -> none  [reduce_padded(): total = term if total is None else total + term]
    concatenate x6 -> x0, other arithmetic: 2.06 us -> none  [extended(): jnp.concatenate([lax.ppermute(tail, axis, [(i, (i + 1) % count) for i in...]
    unnamed x10 -> x3, local copies, waits for them, and re-layouts: 3.43 us -> 4.64 us
  transfers between devices with their start and end apart: 16 -> 0, of which waited for: 6 -> 0; matrix products, arithmetic and copies ran while one was open for 24% -> 0% of each run, Pallas kernels for 0% -> 0%
where the time goes in v1:
time: 27 us; the launch traced here: 26.8 us
  Pallas kernels  21.5 us (80%)
  local copies, waits for them, and re-layouts  4.64 us (17%)
  between operations  0.64 us (2%)
    pallas_call x1, Pallas kernels, on_device(): pl.pallas_call(functools.partial(kernel, sizes, nz, ny, nt), out_shape=tu...  21.5 us
    unnamed x3, local copies, waits for them, and re-layouts  4.64 us

profile of v1, /device:TPU:0, one launch (start us, length us, event | category | flops | bytes accessed | tf_op | source)
XLA Modules:
  0.0 26.8 jit_solution(6574932118104315143)
XLA Ops:
  0.6 21.5 %pyramid.1 = (f32[8,32,512]{2,1,0:T(8,128)}, f32[4,16,256]{2,1,0:T(8,128)}, f32[2,8,128]{2,1,0:T(8,128)}) custom-call(f32[16,64,1024]{2,1,0:T(8,128)} %vol.1), custom_call_target="tpu_custom_call" | custom-call | tf_op jit(solution)/shard_map/pyramid/pallas_call | solution.py:304
  22.1 1.9 %copy.7 = f32[8,32,512]{2,1,0:T(8,128)} copy(f32[8,32,512]{2,1,0:T(8,128)} %get-tuple-element.6) | data formatting | bytes 1048576
  24.0 1.5 %copy.8 = f32[4,16,256]{2,1,0:T(8,128)} copy(f32[4,16,256]{2,1,0:T(8,128)} %get-tuple-element.7) | data formatting | bytes 131072
  25.5 1.3 %copy.9 = f32[2,8,128]{2,1,0:T(8,128)} copy(f32[2,8,128]{2,1,0:T(8,128)} %get-tuple-element.8) | data formatting | bytes 16384

commit v2 on v0

v2 whole, which is shorter than its diff:
```python
import functools

import jax
import jax.numpy as jnp
from jax import lax
from jax.experimental import pallas as pl
from jax.experimental.pallas import tpu as pltpu
from jax.sharding import PartitionSpec as P

LANES = 128
MESH = pl.DeviceIdType.MESH
AXES = ("gz", "gy", "gx")
W0, W1, W2 = 0.0625, 0.25, 0.375


def taps_of(delta):
    far = jnp.abs(delta)
    return jnp.where(
        far == 0, W2, jnp.where(far == 1, W1, jnp.where(far == 2, W0, 0.0))
    ).astype(jnp.bfloat16)


def column_weights():
    row = lax.broadcasted_iota(jnp.int32, (LANES, LANES), 0)
    col = lax.broadcasted_iota(jnp.int32, (LANES, LANES), 1)
    before = taps_of(row - LANES - 2 * col)
    first = taps_of(row - 2 * col)
    second = taps_of(row + LANES - 2 * col)
    after = taps_of(row + 2 * LANES - 2 * col)
    half = LANES // 2
    signed_in = jnp.where(row < half, row, row - LANES)
    signed_out = jnp.where(col < half, col, col - LANES)
    same_side = (row < half) == (col < half)
    halo = taps_of(jnp.where(same_side, signed_in - 2 * signed_out, LANES))
    return before, first, second, after, halo


def split3(x):
    hi = x.astype(jnp.bfloat16)
    rest = x - hi.astype(jnp.float32)
    mid = rest.astype(jnp.bfloat16)
    lo = (rest - mid.astype(jnp.float32)).astype(jnp.bfloat16)
    return hi, mid, lo


def dots(tiles, weights):
    parts = [split3(t) for t in tiles]
    total = None
    for p in (2, 1, 0):
        lhs = jnp.concatenate([q[p] for q in parts], axis=1)
        d = jnp.dot(lhs, weights, preferred_element_type=jnp.float32)
        total = d if total is None else total + d
    return total


def kernel(sizes, nz, ny, nt, vol, out1, out2, out3,
           v, z, zr, ys, yr, t, l1, l2, xs_lo, xs_hi, xr, wm, wh,
           load_sem, zsend, zrecv, ysend, yrecv, xsend, xrecv):
    idx = {a: lax.axis_index(a) for a in AXES}
    has = {}
    near = {}
    for a in AXES:
        has[a, -1], has[a, 1] = idx[a] > 0, idx[a] < sizes[a] - 1
        near[a, -1] = jnp.maximum(idx[a] - 1, 0)
        near[a, 1] = jnp.minimum(idx[a] + 1, sizes[a] - 1)

    def exists(steps):
        found = None
        for a, d in steps.items():
            found = has[a, d] if found is None else jnp.logical_and(found, has[a, d])
        return found

    def device(steps):
        return {a: near[a, d] for a, d in steps.items()}

    groups = ((0, 8), (ny - 8, 8), (8, ny - 16))
    loads = []
    for g, (r0, rn) in enumerate(groups):
        c = pltpu.make_async_copy(
            vol.at[:, pl.ds(r0, rn), :], v.at[:, pl.ds(r0, rn), :], load_sem.at[g])
        c.start()
        loads.append(c)

    xr[...] = jnp.zeros(xr.shape, jnp.float32)
    for lev in range(3):
        yr[lev][...] = jnp.zeros(yr[lev].shape, jnp.float32)

    corners = [{"gz": i, "gy": j} for i in (-1, 1) for j in (-1, 1)]
    peers = [{a: d} for a in AXES for d in (-1, 1)] + corners
    barrier = pltpu.get_barrier_semaphore()
    for p in peers:
        @pl.when(exists(p))
        def _():
            pl.semaphore_signal(barrier, inc=1, device_id=device(p), device_id_type=MESH)

    for lev in range(3):
        rows = z[lev].shape[2] - 16
        edge = jnp.zeros(z[lev].shape[:2] + (8, LANES), jnp.float32)
        z[lev][:, :, 0:8, :] = edge
        z[lev][:, :, 8 + rows:16 + rows, :] = edge
    before, first, second, after, halo = column_weights()
    for i, m in enumerate((before, first, second, after)):
        wm[i * LANES:(i + 1) * LANES] = m
    for i, m in enumerate((before, halo, after)):
        wh[i * LANES:(i + 1) * LANES] = m

    pl.semaphore_wait(barrier, sum(exists(p).astype(jnp.int32) for p in peers))

    sent = []

    def send(steps, src, dst, send_sem, recv_sem):
        copy = pltpu.make_async_remote_copy(
            src_ref=src, dst_ref=dst, send_sem=send_sem, recv_sem=recv_sem,
            device_id=device(steps), device_id_type=MESH)

        @pl.when(exists(steps))
        def _():
            copy.start()
        sent.append((steps, copy))

        def wait():
            @pl.when(exists({a: -d for a, d in steps.items()}))
            def _():
                copy.wait_recv()
        return wait

    def own_sum(load, out, n):
        if isinstance(out, int) and out == n // 2:
            return W0 * load(n - 2) + W1 * load(n - 1)
        if isinstance(out, int) and out == n // 2 + 1:
            return W0 * load(0)
        c = 2 * out
        if isinstance(out, int) and out == 0:
            return W2 * load(c) + W1 * load(c + 1) + W0 * load(c + 2)
        if isinstance(out, int) and out == n // 2 - 1:
            return W0 * load(c - 2) + W1 * (load(c - 1) + load(c + 1)) + W2 * load(c)
        return W0 * (load(c - 2) + load(c + 2)) + W1 * (load(c - 1) + load(c + 1)) + W2 * load(c)

    def sections_first(out, r0, rn):
        for r in range(r0, r0 + rn, 8):
            for lt in range(nt):
                cols = slice(lt * LANES, (lt + 1) * LANES)
                z[0][out, lt, 8 + r:16 + r, :] = own_sum(lambda i: v[i, r:r + 8, cols], out, nz)

    def sections_next(lev, src, out):
        rows = src.shape[2]
        for lt in range(src.shape[1]):
            z[lev][out, lt, 8:8 + rows, :] = own_sum(lambda i: src[i, lt], out, src.shape[0])

    def send_rows(lev):
        zz, snd, rcv = z[lev], ys[lev], yr[lev]
        m, rows = zz.shape[0] - 2, zz.shape[2] - 16
        snd[0] = W0 * zz[:, :, 6 + rows:7 + rows, :] + W1 * zz[:, :, 7 + rows:8 + rows, :]
        snd[1] = W0 * zz[:, :, 8:9, :]
        waits = []
        for i, d in enumerate((1, -1)):
            for k, (steps, part) in enumerate((
                    ({"gy": d}, pl.ds(0, m)),
                    ({"gz": 1, "gy": d}, pl.ds(m, 1)),
                    ({"gz": -1, "gy": d}, pl.ds(m + 1, 1)))):
                waits.append(send(steps, snd.at[i, part], rcv.at[i, part],
                                  ysend.at[6 * lev + 3 * i + k], yrecv.at[6 * lev + 3 * i + k]))
        return waits

    def send_sections(lev):
        zz = z[lev]
        m, rows = zz.shape[0] - 2, zz.shape[2] - 16
        return [
            send({"gz": d}, zz.at[m + i, :, pl.ds(8, rows), :], zr[lev].at[i],
                 zsend.at[2 * lev + i], zrecv.at[2 * lev + i])
            for i, d in enumerate((1, -1))]

    def take_sections(lev, waits):
        zz = z[lev]
        m, rows = zz.shape[0] - 2, zz.shape[2] - 16
        for i, (d, s) in enumerate(((-1, 0), (1, m - 1))):
            waits[i]()

            @pl.when(has["gz", d])
            def _():
                zz[s, :, 8:8 + rows, :] += zr[lev][i]

    def row_sum(lev, s, lt):
        zz = z[lev]
        half = (zz.shape[2] - 16) // 2

        def load(k):
            return zz[s, lt, pl.ds(6 + k, half, 2), :]
        t[lev][lt, s] = W0 * (load(0) + load(4)) + W1 * (load(1) + load(3)) + W2 * load(2)

    def take_rows(lev, lt):
        tt, rcv = t[lev], yr[lev]
        m, rows = tt.shape[1], tt.shape[2]
        for i, r in enumerate((0, rows - 1)):
            for s in range(m):
                add = rcv[i, s, lt]
                if s == 0:
                    add = add + rcv[i, m, lt]
                if s == m - 1:
                    add = add + rcv[i, m + 1, lt]
                tt[lt, s, r:r + 1, :] += add

    def tile_of(tt, i):
        x = tt[i]
        return x.reshape(x.shape[0] * x.shape[1], LANES)

    def main_tile(lev, j):
        tiles = t[lev].shape[0] - 1
        ids = ((2 * j - 1) % (tiles + 1), 2 * j, 2 * j + 1, 2 * j + 2)
        return dots([tile_of(t[lev], i) for i in ids], wm[...])

    def halo_tile(lev):
        tiles = t[lev].shape[0] - 1
        out = dots([tile_of(t[lev], i) for i in (tiles - 1, tiles, 0)], wh[...])
        lane = lax.broadcasted_iota(jnp.int32, out.shape, 1)
        keep_hi = jnp.where(has["gx", 1], 1, 0)
        keep_lo = jnp.where(has["gx", -1], 1, 0)
        keep = jnp.where(lane < LANES // 2, keep_hi, keep_lo)
        return jnp.where(keep > 0, out, 0.0)

    def put(l, j, x):
        l[:, j] = x.reshape(l.shape[0], l.shape[2], LANES)

    def store(l, out):
        for j in range(l.shape[1] - 1):
            out[:, :, j * LANES:(j + 1) * LANES] = l[:, j]

    m, ny1, nt1 = nz // 2, ny // 2, nt // 2
    ends = (0, m - 1, m, m + 1)
    loads[0].wait()
    loads[1].wait()

    @pl.loop(1, m - 1)
    def _(s):
        sections_first(s, 0, 8)
        sections_first(s, ny - 8, 8)
    for s in ends:
        sections_first(s, 0, 8)
        sections_first(s, ny - 8, 8)
    rows_wait = send_rows(0)
    loads[2].wait()
    for s in (m, m + 1):
        sections_first(s, 8, ny - 16)
    sections_wait = send_sections(0)
    for s in (0, m - 1):
        sections_first(s, 8, ny - 16)

    @pl.loop(1, m - 1)
    def _(s):
        sections_first(s, 8, ny - 16)
        for lt in range(nt):
            row_sum(0, s, lt)
    take_sections(0, sections_wait)
    for s in (0, m - 1):
        for lt in range(nt):
            row_sum(0, s, lt)
    for w in rows_wait:
        w()
    take_rows(0, 0)
    take_rows(0, nt - 1)
    xs_lo[...] = tile_of(t[0], 0).T[0:8, :]
    xs_hi[...] = tile_of(t[0], nt - 1).T[LANES - 16:LANES, :]
    columns_wait = [
        send({"gx": 1}, xs_hi, xr.at[pl.ds(LANES - 16, 16)], xsend.at[0], xrecv.at[0]),
        send({"gx": -1}, xs_lo, xr.at[pl.ds(0, 8)], xsend.at[1], xrecv.at[1])]
    for lt in range(1, nt - 1):
        take_rows(0, lt)
    for j in range(1, nt1 - 1):
        put(l1, j, main_tile(0, j))
    for w in columns_wait:
        w()
    t[0][nt] = xr[...].T.reshape(m, ny1, LANES)
    for j in (0, nt1 - 1):
        put(l1, j, main_tile(0, j))
    put(l1, nt1, halo_tile(0))

    for lev, src, out in ((1, l1, out1), (2, l2, out2)):
        m = src.shape[0] // 2
        for s in (m, m + 1):
            sections_next(lev, src, s)
        sections_wait = send_sections(lev)
        for s in range(m):
            sections_next(lev, src, s)
        rows_wait = send_rows(lev)
        store(src, out)
        for s in range(1, m - 1):
            for lt in range(src.shape[1]):
                row_sum(lev, s, lt)
        take_sections(lev, sections_wait)
        for s in (0, m - 1):
            for lt in range(src.shape[1]):
                row_sum(lev, s, lt)
        for w in rows_wait:
            w()
        for lt in range(src.shape[1]):
            take_rows(lev, lt)
        for j in range((src.shape[1] - 1) // 2):
            if lev == 1:
                put(l2, j, main_tile(lev, j))
            else:
                out3[:, :, j * LANES:(j + 1) * LANES] = main_tile(lev, j).reshape(
                    out3.shape[0], out3.shape[1], LANES)
        if lev == 1:
            put(l2, (src.shape[1] - 1) // 2, halo_tile(lev))

    for steps, copy in sent:
        @pl.when(exists(steps))
        def _():
            copy.wait_send()


def write_out(a1, a2, a3, out1, out2, out3, sem):
    copies = [
        pltpu.make_async_copy(src, dst, sem.at[i])
        for i, (src, dst) in enumerate(((a1, out1), (a2, out2), (a3, out3)))]
    for c in copies:
        c.start()
    for c in copies:
        c.wait()


def on_device(sizes, volume):
    f32 = jnp.float32
    nz, ny, nx = volume.shape
    nt = nx // LANES
    V = pltpu.VMEM
    tiles = [nt, (nt >> 1) + 1, (nt >> 2) + 1]
    z = [V((2 + (nz >> (l + 1)), tiles[l], (ny >> l) + 16, LANES), f32) for l in range(3)]
    zr = [V((2, tiles[l], ny >> l, LANES), f32) for l in range(3)]
    y = [V((2, 2 + (nz >> (l + 1)), tiles[l], 1, LANES), f32) for l in range(3)]
    lv = [V((nz >> l, tiles[l], ny >> l, LANES), f32) for l in (1, 2)]
    t = [V(((nt >> l) + 1, nz >> (l + 1), ny >> (l + 1), LANES), f32) for l in range(3)]
    packed = (nz >> 1) * (ny >> 1)
    dma = pltpu.SemaphoreType.DMA
    hbm = pl.BlockSpec(memory_space=pltpu.HBM)
    vmem = pl.BlockSpec(memory_space=pltpu.VMEM)
    volume = pltpu.with_memory_space_constraint(volume, pltpu.HBM)
    levels = pl.pallas_call(
        functools.partial(kernel, sizes, nz, ny, nt),
        out_shape=tuple(
            V((nz >> l, ny >> l, nx >> l), f32) for l in (1, 2, 3)),
        in_specs=[hbm],
        out_specs=(vmem, vmem, vmem),
        scratch_shapes=[
            V((nz, ny, nx), f32), z, zr, y, y, t, *lv,
            V((8, packed), f32), V((16, packed), f32), V((LANES, packed), f32),
            V((4 * LANES, LANES), jnp.bfloat16), V((3 * LANES, LANES), jnp.bfloat16),
            dma((3,)),
            dma((6,)), dma((6,)), dma((18,)), dma((18,)), dma((2,)), dma((2,)),
        ],
        compiler_params=pltpu.CompilerParams(
            collective_id=0, has_side_effects=True, vmem_limit_bytes=40 << 20),
        name="pyramid",
    )(volume)
    return pl.pallas_call(
        write_out,
        out_shape=tuple(jax.ShapeDtypeStruct(x.shape, f32) for x in levels),
        in_specs=[vmem] * 3,
        out_specs=(hbm, hbm, hbm),
        scratch_shapes=[dma((3,))],
        compiler_params=pltpu.CompilerParams(vmem_limit_bytes=4 << 20),
        name="write_out",
    )(*levels)


def solution(mesh):
    sizes = {a: mesh.shape[a] for a in AXES}
    spec = P(*AXES)
    return jax.shard_map(
        functools.partial(on_device, sizes), mesh=mesh, in_specs=(spec,),
        out_specs=(spec, spec, spec), check_vma=False)
```

time: 196 us -> 20.1 us (0.10)
  local copies, waits for them, and re-layouts: 128 us -> 0 us
  starting transfers between devices: 39.6 us -> 0 us
  Pallas kernels: 0 us -> 19.3 us
  waiting for transfers between devices: 16.4 us -> 0 us
  other arithmetic: 7.93 us -> 0 us
    slice x39 -> x0, local copies, waits for them, and re-layouts: 124 us -> none  [the longest x31 122 us: reduce_padded(): piece = lax.slice_in_dim(padded, k, k + 2 * count - 1, 2, dim)]
    ppermute x16 -> x0, starting transfers between devices: 39.6 us -> none  [the longest x8 28.8 us: extended(): lax.ppermute(tail, axis, [(i, (i + 1) % count) for i in range(ends)])]
    pallas_call x0 -> x2, Pallas kernels: none -> 19.3 us  [the longest x1 18.5 us: on_device(): pl.pallas_call(functools.partial(kernel, sizes, nz, ny, nt), out_shape=tu...]
    ppermute x16 -> x0, waiting for transfers between devices: 16.4 us -> none  [the longest x8 16.2 us: extended(): lax.ppermute(head, axis, [((i + 1) % count, i) for i in range(ends)])]
    add x9 -> x0, other arithmetic: 5.87 us -> none  [reduce_padded(): total = term if total is None else total + term]
    unnamed x10 -> x0, local copies, waits for them, and re-layouts: 3.43 us -> none
    concatenate x6 -> x0, other arithmetic: 2.06 us -> none  [extended(): jnp.concatenate([lax.ppermute(tail, axis, [(i, (i + 1) % count) for i in...]
  transfers between devices with their start and end apart: 16 -> 0, of which waited for: 6 -> 0; matrix products, arithmetic and copies ran while one was open for 24% -> 0% of each run, Pallas kernels for 0% -> 0%
where the time goes in v2:
time: 20.1 us; the launch traced here: 20 us
  Pallas kernels  19.3 us (96%)
  between operations  0.64 us (3%)
    pallas_call x1, Pallas kernels, on_device(): pl.pallas_call(functools.partial(kernel, sizes, nz, ny, nt), out_shape=tu...  18.5 us
    pallas_call x1, Pallas kernels, on_device(): pl.pallas_call(write_out, out_shape=tuple((jax.ShapeDtypeStruct(x.shape,...  0.83 us

profile of v2, /device:TPU:0, one launch (start us, length us, event | category | flops | bytes accessed | tf_op | source)
XLA Modules:
  0.0 20.0 jit_solution(9378419521068511890)
XLA Ops:
  0.6 18.5 %pyramid.1 = (f32[8,32,512]{2,1,0:T(8,128)S(1)}, f32[4,16,256]{2,1,0:T(8,128)S(1)}, f32[2,8,128]{2,1,0:T(8,128)S(1)}) custom-call(f32[16,64,1024]{2,1,0:T(8,128)} %vol.1), custom_call_target="tpu_custom_call" | custom-call | tf_op jit(solution)/shard_map/pyramid/pallas_call | solution.py:338
  19.1 0.8 %write_out.1 = (f32[8,32,512]{2,1,0:T(8,128)}, f32[4,16,256]{2,1,0:T(8,128)}, f32[2,8,128]{2,1,0:T(8,128)}) custom-call(f32[8,32,512]{2,1,0:T(8,128)S(1)} %get-tuple-element.6.a1, f32[4,16,256]{2,1,0:T(8,128)S(1)} %get-tuple-element.7.a2, f32[2,8,128]{2,1,0:T(8,128)S(1)} %get-tuple-element.8.a3), custom_call_target="tpu_custom_call" | custom-call | tf_op jit(solution)/shard_map/write_out/pallas_call | solution.py:355

commit v3 on v2

v3 whole, which is shorter than its diff:
```python
import functools

import jax
import jax.numpy as jnp
from jax import lax
from jax.experimental import pallas as pl
from jax.experimental.pallas import tpu as pltpu
from jax.sharding import PartitionSpec as P

LANES = 128
MESH = pl.DeviceIdType.MESH
AXES = ("gz", "gy", "gx")
W0, W1, W2 = 0.0625, 0.25, 0.375


def taps_of(delta):
    far = jnp.abs(delta)
    return jnp.where(
        far == 0, W2, jnp.where(far == 1, W1, jnp.where(far == 2, W0, 0.0))
    ).astype(jnp.bfloat16)


def column_weights():
    row = lax.broadcasted_iota(jnp.int32, (LANES, LANES), 0)
    col = lax.broadcasted_iota(jnp.int32, (LANES, LANES), 1)
    before = taps_of(row - LANES - 2 * col)
    first = taps_of(row - 2 * col)
    second = taps_of(row + LANES - 2 * col)
    after = taps_of(row + 2 * LANES - 2 * col)
    half = LANES // 2
    signed_in = jnp.where(row < half, row, row - LANES)
    signed_out = jnp.where(col < half, col, col - LANES)
    same_side = (row < half) == (col < half)
    halo = taps_of(jnp.where(same_side, signed_in - 2 * signed_out, LANES))
    return before, first, second, after, halo


def split3(x):
    hi = x.astype(jnp.bfloat16)
    rest = x - hi.astype(jnp.float32)
    mid = rest.astype(jnp.bfloat16)
    lo = (rest - mid.astype(jnp.float32)).astype(jnp.bfloat16)
    return hi, mid, lo


def dots(tiles, weights):
    parts = [split3(t) for t in tiles]
    total = None
    for p in (2, 1, 0):
        lhs = jnp.concatenate([q[p] for q in parts], axis=1)
        d = jnp.dot(lhs, weights, preferred_element_type=jnp.float32)
        total = d if total is None else total + d
    return total


def kernel(sizes, dims, vol, out1, out2, out3,
           v, z, t, sh, rz_lo, rz_hi, ys_lo, ys_hi, yr_lo, yr_hi, xs, xr, wm, wh,
           load_sem, zsend, zrecv, ysend, yrecv, xsend, xrecv):
    nz, ny, nt = dims
    idx = {a: lax.axis_index(a) for a in AXES}
    has = {}
    near = {}
    for a in AXES:
        has[a, -1], has[a, 1] = idx[a] > 0, idx[a] < sizes[a] - 1
        near[a, -1] = jnp.maximum(idx[a] - 1, 0)
        near[a, 1] = jnp.minimum(idx[a] + 1, sizes[a] - 1)

    def flag(a, d):
        return jnp.where(has[a, d], 1.0, 0.0).astype(jnp.float32)

    def exists(steps):
        found = None
        for a, d in steps.items():
            found = has[a, d] if found is None else jnp.logical_and(found, has[a, d])
        return found

    def device(steps):
        return {a: near[a, d] for a, d in steps.items()}

    groups = ((0, ny // 2), (ny // 2, ny // 2))
    loads = []
    for g, (r0, rn) in enumerate(groups):
        c = pltpu.make_async_copy(
            vol.at[:, pl.ds(r0, rn), :], v.at[:, pl.ds(r0, rn), :], load_sem.at[g])
        c.start()
        loads.append(c)

    xr[...] = jnp.zeros(xr.shape, jnp.float32)
    for lev in range(3):
        yr_lo[lev][...] = jnp.zeros(yr_lo[lev].shape, jnp.float32)
        yr_hi[lev][...] = jnp.zeros(yr_hi[lev].shape, jnp.float32)

    corners = [{"gz": i, "gy": j} for i in (-1, 1) for j in (-1, 1)]
    peers = [{a: d} for a in AXES for d in (-1, 1)] + corners
    barrier = pltpu.get_barrier_semaphore()
    for p in peers:
        @pl.when(exists(p))
        def _():
            pl.semaphore_signal(barrier, inc=1, device_id=device(p), device_id_type=MESH)

    for lev in range(3):
        pad = z[lev].shape[:2]
        rows = z[lev].shape[2] - 32
        first_pad = 8 + rows if lev == 0 else 16 + rows
        if lev == 0:
            z[lev][:, :, 0:8, :] = jnp.zeros(pad + (8, LANES), jnp.float32)
        z[lev][:, :, first_pad:32 + rows, :] = jnp.zeros(
            pad + (32 + rows - first_pad, LANES), jnp.float32)
    before, first, second, after, halo = column_weights()
    for i, m in enumerate((before, first, second, after)):
        wm[i * LANES:(i + 1) * LANES] = m
    for i, m in enumerate((before, halo, after)):
        wh[i * LANES:(i + 1) * LANES] = m

    sent = []

    def send(steps, src, dst, send_sem, recv_sem):
        copy = pltpu.make_async_remote_copy(
            src_ref=src, dst_ref=dst, send_sem=send_sem, recv_sem=recv_sem,
            device_id=device(steps), device_id_type=MESH)

        @pl.when(exists(steps))
        def _():
            copy.start()
        sent.append((steps, copy))

        def wait():
            @pl.when(exists({a: -d for a, d in steps.items()}))
            def _():
                copy.wait_recv()
        return wait

    tap = {0: W2, 1: W1, 2: W0}
    fz_lo, fz_hi = flag("gz", -1), flag("gz", 1)
    fy_lo, fy_hi = flag("gy", -1), flag("gy", 1)

    def own_sum(load, o, n, ghosts_hi, last):
        if not isinstance(o, int):
            c = 2 * o
            return W0 * (load(c - 2) + load(c + 2)) + W1 * (load(c - 1) + load(c + 1)) \
                + W2 * load(c)
        total = None
        for i in range(2 * o - 2, 2 * o + 3):
            if i < (-1 if ghosts_hi else 0) or i >= n + ghosts_hi:
                continue
            term = tap[abs(i - 2 * o)] * load(i if i >= 0 else last)
            total = term if total is None else total + term
        if o < 0:
            total = total * fz_lo
        elif o >= n // 2:
            total = total * fz_hi
        return total

    def row_sum(lev, s, lt):
        zz = z[lev]
        half = (zz.shape[2] - 32) // 2

        def load(k):
            return zz[s, lt, pl.ds(6 + k, half + 8, 2), :]
        x = W0 * (load(0) + load(4)) + W1 * (load(1) + load(3)) + W2 * load(2)
        lo = (W1 * zz[s, lt, 7:8, :] + W0 * zz[s, lt, 8:9, :]) * fy_lo
        row = lax.broadcasted_iota(jnp.int32, (8, LANES), 0)
        ghost = jnp.where(row < 2, x[half:half + 8] * fy_hi, jnp.where(row == 7, lo, 0.0))
        t[lev][lt, s, 0:half, :] = x[0:half]
        t[lev][lt, s, half:half + 8, :] = ghost

    def tile_of(tt, i):
        x = tt[i]
        return x.reshape(x.shape[0] * x.shape[1], LANES)

    def put(lev, j, x):
        out = sh[lev]
        out[:, j] = x.reshape(out.shape[0], out.shape[2], LANES)

    def columns(lev, tiles):
        tt = t[lev]
        for j in range(tiles // 2):
            ids = [2 * j - 1, 2 * j, 2 * j + 1, 2 * j + 2]
            lo, hi = 0, 4
            if j == 0:
                ids[0] = tiles
                lo = 1 if lev == 0 else 0
            if j == tiles // 2 - 1 and lev == 0:
                hi = 3
            put(lev, j, dots([tile_of(tt, i) for i in ids[lo:hi]], wm[lo * LANES:hi * LANES]))
        if lev == 0:
            w = jnp.concatenate([wh[0:LANES], wh[2 * LANES:3 * LANES]], axis=0)
            out = dots([tile_of(tt, tiles - 1), tile_of(tt, 0)], w)
        else:
            out = dots([tile_of(tt, i) for i in (tiles - 1, tiles, 0)], wh[...])
        lane = lax.broadcasted_iota(jnp.int32, out.shape, 1)
        keep_hi = jnp.where(has["gx", 1], 1, 0)
        keep_lo = jnp.where(has["gx", -1], 1, 0)
        keep = jnp.where(lane < LANES // 2, keep_hi, keep_lo)
        put(lev, tiles // 2, jnp.where(keep > 0, out, 0.0))

    def send_shares(lev):
        s = sh[lev]
        n, rows = nz >> (lev + 1), s.shape[2] - 8
        g = s.shape[0] - n - 1
        ys_hi[lev][...] = s[:, :, rows:rows + g, :]
        ys_lo[lev][...] = s[:, :, rows + 7:rows + 8, :]
        ups, downs, sections = [], [], []
        for i, (d, snd, rcv, waits) in enumerate((
                (1, ys_hi[lev], yr_lo[lev], ups), (-1, ys_lo[lev], yr_hi[lev], downs))):
            for k, (steps, part) in enumerate((
                    ({"gy": d}, pl.ds(0, n)),
                    ({"gz": 1, "gy": d}, pl.ds(n, g)),
                    ({"gz": -1, "gy": d}, pl.ds(n + g, 1)))):
                at = 6 * lev + 3 * i + k
                waits.append(send(steps, snd.at[part], rcv.at[part], ysend.at[at], yrecv.at[at]))
        sections.append(send(
            {"gz": 1}, s.at[pl.ds(n, g), :, pl.ds(0, rows), :], rz_lo[lev],
            zsend.at[2 * lev], zrecv.at[2 * lev]))
        sections.append(send(
            {"gz": -1}, s.at[pl.ds(n + g, 1), :, pl.ds(0, rows), :], rz_hi[lev],
            zsend.at[2 * lev + 1], zrecv.at[2 * lev + 1]))
        return sections, ups + downs

    def take_sections(lev, waits):
        s = sh[lev]
        n, rows = nz >> (lev + 1), s.shape[2] - 8
        g = s.shape[0] - n - 1
        waits[0]()

        @pl.when(has["gz", -1])
        def _():
            s[0:g, :, 0:rows, :] += rz_lo[lev][...]
        waits[1]()

        @pl.when(has["gz", 1])
        def _():
            s[n - 1:n, :, 0:rows, :] += rz_hi[lev][...]

    def take_rows(lev, waits):
        s = sh[lev]
        n, rows = nz >> (lev + 1), s.shape[2] - 8
        g = s.shape[0] - n - 1
        for w in waits:
            w()
        for rcv, r, h in ((yr_lo[lev], 0, g), (yr_hi[lev], rows - 1, 1)):
            for i in range(n):
                add = rcv[i]
                if i < g:
                    add = add + rcv[n + i]
                if i == n - 1:
                    add = add + rcv[n + g]
                s[i, :, r:r + h, :] += add

    m = nz // 2

    def sections_first(o, at, r0, rn):
        for r in range(r0, r0 + rn, 8):
            for lt in range(nt):
                cols = slice(lt * LANES, (lt + 1) * LANES)
                z[0][at, lt, 8 + r:16 + r, :] = own_sum(
                    lambda i: v[i, r:r + 8, cols], o, nz, 0, 0)

    for c, (r0, rn) in zip(loads, groups):
        c.wait()

        @pl.loop(1, m - 1)
        def _(o):
            sections_first(o, o, r0, rn)
        for o, at in ((0, 0), (m - 1, m - 1), (m, m), (-1, m + 1)):
            sections_first(o, at, r0, rn)

    @pl.loop(0, m + 2)
    def _(o):
        for lt in range(nt):
            row_sum(0, o, lt)
    columns(0, nt)
    pl.semaphore_wait(barrier, sum(exists(p).astype(jnp.int32) for p in peers))
    waits = [send_shares(0)]

    for lev in (1, 2):
        src = sh[lev - 1]
        n = nz >> lev
        rows = src.shape[2] - 8
        g = src.shape[0] - n - 1
        tiles = src.shape[1] - 1
        outs = [(o, o) for o in range(n // 2 + 2)] + [(-1, n // 2 + 2)]
        for o, at in outs:
            for lt in range(tiles + 1):
                x = own_sum(lambda i: src[i, lt], o, n, g, n + g)
                z[lev][at, lt, 8:16 + rows, :] = x
                z[lev][at, lt, 0:8, :] = x[rows:rows + 8]
        for o, at in outs:
            for lt in range(tiles + 1):
                row_sum(lev, at, lt)
        columns(lev, tiles)
        waits.append(send_shares(lev))

    for lev in range(3):
        take_sections(lev, waits[lev][0])
    for lev in range(3):
        take_rows(lev, waits[lev][1])
    outs = (out1, out2, out3)
    flat = []
    for lev in range(3):
        n, rows, last = nz >> (lev + 1), sh[lev].shape[2] - 8, sh[lev].shape[1] - 1
        flat.append(sh[lev][0:n, last, 0:rows, :].reshape(n * rows, LANES))
    used = sum(f.shape[0] for f in flat)
    if xr.shape[1] > used:
        flat.append(jnp.zeros((xr.shape[1] - used, LANES), jnp.float32))
    packed = jnp.concatenate(flat, axis=0).T
    xs[0:8, :] = packed[0:8, :]
    xs[8:16, :] = packed[LANES - 8:LANES, :]
    columns_wait = [
        send({"gx": 1}, xs.at[pl.ds(0, 8)], xr.at[pl.ds(0, 8)], xsend.at[0], xrecv.at[0]),
        send({"gx": -1}, xs.at[pl.ds(8, 8)], xr.at[pl.ds(LANES - 8, 8)], xsend.at[1],
             xrecv.at[1])]

    def store(lev, j, x):
        outs[lev][:, :, j * LANES:(j + 1) * LANES] = x

    for lev in range(3):
        n, rows, count = nz >> (lev + 1), sh[lev].shape[2] - 8, sh[lev].shape[1] - 1
        for j in range(1, count - 1):
            store(lev, j, sh[lev][0:n, j, 0:rows, :])
    for w in columns_wait:
        w()
    back = xr[...].T
    start = 0
    for lev in range(3):
        n, rows, count = nz >> (lev + 1), sh[lev].shape[2] - 8, sh[lev].shape[1] - 1
        add = back[start:start + n * rows].reshape(n, rows, LANES)
        start += n * rows
        lane = lax.broadcasted_iota(jnp.int32, add.shape, 2)
        at_lo = jnp.where(lane < 2, add, 0.0)
        at_hi = jnp.where(lane == LANES - 1, add, 0.0)
        x = sh[lev][0:n, 0, 0:rows, :] + at_lo
        if count == 1:
            store(lev, 0, x + at_hi)
        else:
            store(lev, 0, x)
            store(lev, count - 1, sh[lev][0:n, count - 1, 0:rows, :] + at_hi)

    for steps, copy in sent:
        @pl.when(exists(steps))
        def _():
            copy.wait_send()


def write_out(a1, a2, a3, out1, out2, out3, sem):
    copies = [
        pltpu.make_async_copy(src, dst, sem.at[i])
        for i, (src, dst) in enumerate(((a1, out1), (a2, out2), (a3, out3)))]
    for c in copies:
        c.start()
    for c in copies:
        c.wait()


def on_device(sizes, volume):
    f32 = jnp.float32
    nz, ny, nx = volume.shape
    nt = nx // LANES
    V = pltpu.VMEM
    extra = (2, 3, 3)
    ins = (nt, (nt >> 1) + 1, (nt >> 2) + 1)
    n = [nz >> (l + 1) for l in range(3)]
    rows = [ny >> (l + 1) for l in range(3)]
    outs = [(nt >> (l + 1)) + 1 for l in range(3)]
    levels = range(3)
    z = [V((n[l] + extra[l], ins[l], 2 * rows[l] + 32, LANES), f32) for l in levels]
    t = [V((ins[l], n[l] + extra[l], rows[l] + 8, LANES), f32) for l in levels]
    sh = [V((n[l] + extra[l], outs[l], rows[l] + 8, LANES), f32) for l in levels]
    rz_lo = [V((extra[l] - 1, outs[l], rows[l], LANES), f32) for l in levels]
    rz_hi = [V((1, outs[l], rows[l], LANES), f32) for l in levels]
    lows = [V((n[l] + extra[l], outs[l], 1, LANES), f32) for l in levels]
    highs = [V((n[l] + extra[l], outs[l], extra[l] - 1, LANES), f32) for l in levels]
    packed = -(-sum(n[l] * rows[l] for l in levels) // LANES) * LANES
    dma = pltpu.SemaphoreType.DMA
    hbm = pl.BlockSpec(memory_space=pltpu.HBM)
    vmem = pl.BlockSpec(memory_space=pltpu.VMEM)
    volume = pltpu.with_memory_space_constraint(volume, pltpu.HBM)
    results = pl.pallas_call(
        functools.partial(kernel, sizes, (nz, ny, nt)),
        out_shape=tuple(
            V((nz >> l, ny >> l, nx >> l), f32) for l in (1, 2, 3)),
        in_specs=[hbm],
        out_specs=(vmem, vmem, vmem),
        scratch_shapes=[
            V((nz, ny, nx), f32), z, t, sh, rz_lo, rz_hi, lows, highs, highs, lows,
            V((16, packed), f32), V((LANES, packed), f32),
            V((4 * LANES, LANES), jnp.bfloat16), V((3 * LANES, LANES), jnp.bfloat16),
            dma((3,)),
            dma((6,)), dma((6,)), dma((18,)), dma((18,)), dma((2,)), dma((2,)),
        ],
        compiler_params=pltpu.CompilerParams(
            collective_id=0, has_side_effects=True, vmem_limit_bytes=40 << 20),
        name="pyramid",
    )(volume)
    return pl.pallas_call(
        write_out,
        out_shape=tuple(jax.ShapeDtypeStruct(x.shape, f32) for x in results),
        in_specs=[vmem] * 3,
        out_specs=(hbm, hbm, hbm),
        scratch_shapes=[dma((3,))],
        compiler_params=pltpu.CompilerParams(vmem_limit_bytes=4 << 20),
        name="write_out",
    )(*results)


def solution(mesh):
    sizes = {a: mesh.shape[a] for a in AXES}
    spec = P(*AXES)
    return jax.shard_map(
        functools.partial(on_device, sizes), mesh=mesh, in_specs=(spec,),
        out_specs=(spec, spec, spec), check_vma=False)
```

time: 20.1 us -> 16.6 us (0.83)
  Pallas kernels: 19.3 us -> 15.9 us
    pallas_call x1, Pallas kernels: 18.5 us -> 15 us  [on_device(): pl.pallas_call(functools.partial(kernel, sizes, (nz, ny, nt)), out_shape=...]
where the time goes in v3:
time: 16.6 us; the launch traced here: 16.5 us
  Pallas kernels  15.9 us (96%)
  between operations  0.64 us (4%)
    pallas_call x1, Pallas kernels, on_device(): pl.pallas_call(functools.partial(kernel, sizes, (nz, ny, nt)), out_shape=...  15 us
    pallas_call x1, Pallas kernels, on_device(): pl.pallas_call(write_out, out_shape=tuple((jax.ShapeDtypeStruct(x.shape,...  0.83 us

profile of v3, /device:TPU:0, one launch (start us, length us, event | category | flops | bytes accessed | tf_op | source)
XLA Modules:
  0.0 16.5 jit_solution(7228608578519883389)
XLA Ops:
  0.6 15.0 %pyramid.1 = (f32[8,32,512]{2,1,0:T(8,128)S(1)}, f32[4,16,256]{2,1,0:T(8,128)S(1)}, f32[2,8,128]{2,1,0:T(8,128)S(1)}) custom-call(f32[16,64,1024]{2,1,0:T(8,128)} %vol.1), custom_call_target="tpu_custom_call" | custom-call | tf_op jit(solution)/shard_map/pyramid/pallas_call | solution.py:378
  15.7 0.8 %write_out.1 = (f32[8,32,512]{2,1,0:T(8,128)}, f32[4,16,256]{2,1,0:T(8,128)}, f32[2,8,128]{2,1,0:T(8,128)}) custom-call(f32[8,32,512]{2,1,0:T(8,128)S(1)} %get-tuple-element.6.a1, f32[4,16,256]{2,1,0:T(8,128)S(1)} %get-tuple-element.7.a2, f32[2,8,128]{2,1,0:T(8,128)S(1)} %get-tuple-element.8.a3), custom_call_target="tpu_custom_call" | custom-call | tf_op jit(solution)/shard_map/write_out/pallas_call | solution.py:395

commit v4 on v3

--- a/solution.py
+++ b/solution.py
@@ -43,8 +43,7 @@
     return hi, mid, lo
 
 
-def dots(tiles, weights):
-    parts = [split3(t) for t in tiles]
+def dots(parts, weights):
     total = None
     for p in (2, 1, 0):
         lhs = jnp.concatenate([q[p] for q in parts], axis=1)
@@ -77,7 +76,8 @@
     def device(steps):
         return {a: near[a, d] for a, d in steps.items()}
 
-    groups = ((0, ny // 2), (ny // 2, ny // 2))
+    step = 16 if ny % 16 == 0 else 8
+    groups = [(r, step) for r in range(0, ny, step)]
     loads = []
     for g, (r0, rn) in enumerate(groups):
         c = pltpu.make_async_copy(
@@ -174,6 +174,7 @@
 
     def columns(lev, tiles):
         tt = t[lev]
+        parts = [split3(tile_of(tt, i)) for i in range(tt.shape[0])]
         for j in range(tiles // 2):
             ids = [2 * j - 1, 2 * j, 2 * j + 1, 2 * j + 2]
             lo, hi = 0, 4
@@ -182,12 +183,12 @@
                 lo = 1 if lev == 0 else 0
             if j == tiles // 2 - 1 and lev == 0:
                 hi = 3
-            put(lev, j, dots([tile_of(tt, i) for i in ids[lo:hi]], wm[lo * LANES:hi * LANES]))
+            put(lev, j, dots([parts[i] for i in ids[lo:hi]], wm[lo * LANES:hi * LANES]))
         if lev == 0:
             w = jnp.concatenate([wh[0:LANES], wh[2 * LANES:3 * LANES]], axis=0)
-            out = dots([tile_of(tt, tiles - 1), tile_of(tt, 0)], w)
+            out = dots([parts[tiles - 1], parts[0]], w)
         else:
-            out = dots([tile_of(tt, i) for i in (tiles - 1, tiles, 0)], wh[...])
+            out = dots([parts[i] for i in (tiles - 1, tiles, 0)], wh[...])
         lane = lax.broadcasted_iota(jnp.int32, out.shape, 1)
         keep_hi = jnp.where(has["gx", 1], 1, 0)
         keep_lo = jnp.where(has["gx", -1], 1, 0)
@@ -217,35 +218,31 @@
             zsend.at[2 * lev + 1], zrecv.at[2 * lev + 1]))
         return sections, ups + downs
 
-    def take_sections(lev, waits):
+    def take_sections(lev, tiles):
         s = sh[lev]
         n, rows = nz >> (lev + 1), s.shape[2] - 8
         g = s.shape[0] - n - 1
-        waits[0]()
 
         @pl.when(has["gz", -1])
         def _():
-            s[0:g, :, 0:rows, :] += rz_lo[lev][...]
-        waits[1]()
+            s[0:g, tiles, 0:rows, :] += rz_lo[lev][:, tiles]
 
         @pl.when(has["gz", 1])
         def _():
-            s[n - 1:n, :, 0:rows, :] += rz_hi[lev][...]
-
-    def take_rows(lev, waits):
+            s[n - 1:n, tiles, 0:rows, :] += rz_hi[lev][:, tiles]
+
+    def take_rows(lev, tiles):
         s = sh[lev]
         n, rows = nz >> (lev + 1), s.shape[2] - 8
         g = s.shape[0] - n - 1
-        for w in waits:
-            w()
         for rcv, r, h in ((yr_lo[lev], 0, g), (yr_hi[lev], rows - 1, 1)):
             for i in range(n):
-                add = rcv[i]
+                add = rcv[i, tiles]
                 if i < g:
-                    add = add + rcv[n + i]
+                    add = add + rcv[n + i, tiles]
                 if i == n - 1:
-                    add = add + rcv[n + g]
-                s[i, :, r:r + h, :] += add
+                    add = add + rcv[n + g, tiles]
+                s[i, tiles, r:r + h, :] += add
 
     m = nz // 2
 
@@ -292,9 +289,13 @@
         waits.append(send_shares(lev))
 
     for lev in range(3):
-        take_sections(lev, waits[lev][0])
-    for lev in range(3):
-        take_rows(lev, waits[lev][1])
+        for w in waits[lev][0]:
+            w()
+        take_sections(lev, pl.ds(sh[lev].shape[1] - 1, 1))
+    for lev in range(3):
+        for w in waits[lev][1]:
+            w()
+        take_rows(lev, pl.ds(sh[lev].shape[1] - 1, 1))
     outs = (out1, out2, out3)
     flat = []
     for lev in range(3):
@@ -310,6 +311,10 @@
         send({"gx": 1}, xs.at[pl.ds(0, 8)], xr.at[pl.ds(0, 8)], xsend.at[0], xrecv.at[0]),
         send({"gx": -1}, xs.at[pl.ds(8, 8)], xr.at[pl.ds(LANES - 8, 8)], xsend.at[1],
              xrecv.at[1])]
+
+    for lev in range(3):
+        take_sections(lev, pl.ds(0, sh[lev].shape[1] - 1))
+        take_rows(lev, pl.ds(0, sh[lev].shape[1] - 1))
 
     def store(lev, j, x):
         outs[lev][:, :, j * LANES:(j + 1) * LANES] = x
@@ -385,7 +390,7 @@
             V((nz, ny, nx), f32), z, t, sh, rz_lo, rz_hi, lows, highs, highs, lows,
             V((16, packed), f32), V((LANES, packed), f32),
             V((4 * LANES, LANES), jnp.bfloat16), V((3 * LANES, LANES), jnp.bfloat16),
-            dma((3,)),
+            dma((ny // 8,)),
             dma((6,)), dma((6,)), dma((18,)), dma((18,)), dma((2,)), dma((2,)),
         ],
         compiler_params=pltpu.CompilerParams(

time: 16.6 us -> 16.5 us (level)
  Pallas kernels: 15.9 us -> 15.7 us
where the time goes in v4:
time: 16.5 us; the launch traced here: 16.3 us
  Pallas kernels  15.7 us (95%)
  between operations  0.64 us (4%)
    pallas_call x1, Pallas kernels, on_device(): pl.pallas_call(functools.partial(kernel, sizes, (nz, ny, nt)), out_shape=...  14.9 us
    pallas_call x1, Pallas kernels, on_device(): pl.pallas_call(write_out, out_shape=tuple((jax.ShapeDtypeStruct(x.shape,...  0.83 us

profile of v4, /device:TPU:0, one launch (start us, length us, event | category | flops | bytes accessed | tf_op | source)
XLA Modules:
  0.0 16.3 jit_solution(17175287999727390227)
XLA Ops:
  0.6 14.9 %pyramid.1 = (f32[8,32,512]{2,1,0:T(8,128)S(1)}, f32[4,16,256]{2,1,0:T(8,128)S(1)}, f32[2,8,128]{2,1,0:T(8,128)S(1)}) custom-call(f32[16,64,1024]{2,1,0:T(8,128)} %vol.1), custom_call_target="tpu_custom_call" | custom-call | tf_op jit(solution)/shard_map/pyramid/pallas_call | solution.py:383
  15.5 0.8 %write_out.1 = (f32[8,32,512]{2,1,0:T(8,128)}, f32[4,16,256]{2,1,0:T(8,128)}, f32[2,8,128]{2,1,0:T(8,128)}) custom-call(f32[8,32,512]{2,1,0:T(8,128)S(1)} %get-tuple-element.6.a1, f32[4,16,256]{2,1,0:T(8,128)S(1)} %get-tuple-element.7.a2, f32[2,8,128]{2,1,0:T(8,128)S(1)} %get-tuple-element.8.a3), custom_call_target="tpu_custom_call" | custom-call | tf_op jit(solution)/shard_map/write_out/pallas_call | solution.py:400
